TPU v7x, 32 devices: a whole 2x2x4 slice. The times are simulated.
32 devices in a mesh: cand: 4 (over y, core), tensor: 8 (over z, x).
Axes of the slice: x: 2, y: 2, z: 4, core: 2. Of those that a mesh axis runs over, the one named last changes fastest.
Arguments:
- states: bfloat16 [512, 3584], P('cand'), may hold values from -60 to 60
- targets: int32 [512], replicated, may hold values from 0 to 131071
- loss_mask: int32 [512], P('cand'), may hold values 0 or 1
- cand_of: int32 [4], replicated, may hold values from 0 to 3
- lambdas: float32 [4], replicated, may hold values from 0.2 to 1
- base_q: bfloat16 [3584, 4096], P('cand', 'tensor'), may hold values from -0.09375 to 0.09375
- delta_q: bfloat16 [2, 3584, 4096], P(None, 'cand', 'tensor'), may hold values from -0.046875 to 0.046875
- base_k: bfloat16 [3584, 2048], P('cand'), may hold values from -0.09375 to 0.09375
- delta_k: bfloat16 [2, 3584, 2048], P(None, 'cand'), may hold values from -0.046875 to 0.046875
- base_v: bfloat16 [3584, 2048], P('cand'), may hold values from -0.09375 to 0.09375
- delta_v: bfloat16 [2, 3584, 2048], P(None, 'cand'), may hold values from -0.046875 to 0.046875
- base_o: bfloat16 [4096, 3584], P('tensor', 'cand'), may hold values from -0.09375 to 0.09375
- delta_o: bfloat16 [2, 4096, 3584], P(None, 'tensor', 'cand'), may hold values from -0.046875 to 0.046875
- pre_gain: float32 [3584], replicated, may hold values from 0.5 to 2
- post_gain: float32 [3584], replicated, may hold values from 0.5 to 2
- final_gain: float32 [3584], replicated, may hold values from 0.5 to 2
- unembed: bfloat16 [3584, 131072], P(None, ('cand', 'tensor')), may hold values from -0.3125 to 0.3125
Outputs:
- token_loss: float32 [512], P('cand')
- cand_loss: float32 [4], replicated
All inputs are finite; a program needn't handle non-finite values. No bound on the sum of `loss_mask` on one device may be relied on, other than what follows from the above.
Results may differ from a plain program's by a relative error of at most 0.002.
Values may be sent and summed in bfloat16 or wider, within the bound.
No kernel may reach another device: no remote copies, remote signals or barrier semaphores. Data moves between devices by JAX's collectives and lax.ppermute only.
A program may use at most 128 MiB of HBM per device.

v0:
```python
import math
import jax
import jax.numpy as jnp
from jax import lax
from jax.sharding import PartitionSpec as P

KV = 8
HEAD_SIZE = 256
CANDS = 4


def root_norm(entries, scale_gain):
    mean_square = jnp.mean(entries * entries, axis=-1, keepdims=True)
    return entries * lax.rsqrt(mean_square + 1e-06) * scale_gain


def rotate_pairs(entries, length):
    half_width = entries.shape[-1] // 2
    positions = jnp.arange(length).astype(jnp.float32)
    frequency = jnp.exp(
        -math.log(10000.0) * jnp.arange(half_width).astype(jnp.float32) * 2.0 / entries.shape[-1]
    )
    angles = positions[:, None] * frequency[None, :]
    cosine = jnp.cos(angles)[:, None, :]
    sine_part = jnp.sin(angles)[:, None, :]
    first = entries[..., :half_width]
    second = entries[..., half_width:]
    return jnp.concatenate(
        [first * cosine - second * sine_part, second * cosine + first * sine_part], axis=-1
    )


def task_total(delta):
    return jnp.sum(delta.astype(jnp.float32), axis=0).astype(jnp.bfloat16)


def merge_weights(base, total, mixing):
    return (base.astype(jnp.float32) + mixing * total.astype(jnp.float32)).astype(jnp.bfloat16)


def on_device(
    states,
    targets,
    loss_mask,
    cand_of,
    lambdas,
    base_q,
    delta_q,
    base_k,
    delta_k,
    base_v,
    delta_v,
    base_o,
    delta_o,
    pre_gain,
    post_gain,
    final_gain,
    unembed,
):
    cand_id = lax.axis_index("cand")
    tensor_id = lax.axis_index("tensor")
    tensor_count = lax.axis_size("tensor")
    chosen = cand_of[cand_id]
    mixing = lambdas[chosen]
    group_size = tensor_count // KV
    head_start = tensor_id // group_size * HEAD_SIZE
    own_base_k = lax.dynamic_slice_in_dim(base_k, head_start, HEAD_SIZE, 1)
    own_base_v = lax.dynamic_slice_in_dim(base_v, head_start, HEAD_SIZE, 1)
    own_delta_k = lax.dynamic_slice_in_dim(delta_k, head_start, HEAD_SIZE, 2)
    own_delta_v = lax.dynamic_slice_in_dim(delta_v, head_start, HEAD_SIZE, 2)
    summed = [task_total(delta) for delta in (delta_q, own_delta_k, own_delta_v, delta_o)]
    pieces = (
        lax.all_gather(base_q, "cand", axis=0, tiled=True),
        lax.all_gather(own_base_k, "cand", axis=0, tiled=True),
        lax.all_gather(own_base_v, "cand", axis=0, tiled=True),
        lax.all_gather(base_o, "cand", axis=1, tiled=True),
        lax.all_gather(summed[0], "cand", axis=0, tiled=True),
        lax.all_gather(summed[1], "cand", axis=0, tiled=True),
        lax.all_gather(summed[2], "cand", axis=0, tiled=True),
        lax.all_gather(summed[3], "cand", axis=1, tiled=True),
    )
    base_parts = pieces[:4]
    task_parts = pieces[4:]
    w_query = merge_weights(base_parts[0], task_parts[0], mixing)
    w_key = merge_weights(base_parts[1], task_parts[1], mixing)
    w_value = merge_weights(base_parts[2], task_parts[2], mixing)
    w_out = merge_weights(base_parts[3], task_parts[3], mixing)
    length = states.shape[0]
    stream = states.astype(jnp.float32)
    normed = root_norm(stream, pre_gain).astype(jnp.bfloat16)
    query_rows = jnp.dot(normed, w_query, preferred_element_type=jnp.float32).reshape(
        length, -1, HEAD_SIZE
    )
    query_rows = rotate_pairs(query_rows, length).astype(jnp.bfloat16)
    key_full = jnp.dot(normed, w_key, preferred_element_type=jnp.float32).astype(jnp.bfloat16)
    value_full = jnp.dot(normed, w_value, preferred_element_type=jnp.float32).astype(jnp.bfloat16)
    key_matrix = rotate_pairs(
        key_full.astype(jnp.float32).reshape(length, 1, HEAD_SIZE), length
    ).astype(jnp.bfloat16)[:, 0, :]
    attention_scores = jnp.einsum(
        "lhd,md->hlm", query_rows, key_matrix, preferred_element_type=jnp.float32
    ) * HEAD_SIZE ** (-0.5)
    attention_scores = 50.0 * jnp.tanh(attention_scores / 50.0)
    causal = jnp.arange(length)[:, None] >= jnp.arange(length)[None, :]
    weights = jnp.where(causal[None, :, :], jnp.exp(attention_scores), 0.0)
    attention_probs = (weights / jnp.sum(weights, axis=-1, keepdims=True)).astype(jnp.bfloat16)
    context_rows = jnp.einsum(
        "hlm,md->lhd", attention_probs, value_full, preferred_element_type=jnp.float32
    )
    context_rows = context_rows.astype(jnp.bfloat16).reshape(length, -1)
    partial_value = jnp.dot(context_rows, w_out, preferred_element_type=jnp.float32)
    vocab_width = unembed.shape[1]
    vocab_start = (cand_id * tensor_count + tensor_id) * vocab_width
    vocab_index = jnp.arange(vocab_width)
    attended = lax.psum(partial_value, "tensor")
    final_rows = root_norm(stream + root_norm(attended, post_gain), final_gain).astype(jnp.bfloat16)
    logits = jnp.dot(
        lax.all_gather(final_rows, "cand", axis=0, tiled=True),
        unembed,
        preferred_element_type=jnp.float32,
    )
    capped = 30.0 * jnp.tanh(logits / 30.0)
    totals = jnp.sum(jnp.exp(capped), axis=1)
    local_ids = targets - vocab_start
    matches = local_ids[:, None] == vocab_index[None, :]
    picked = jnp.sum(jnp.where(matches, capped, 0.0), axis=1)
    vocab_sums = jnp.stack([totals, picked], axis=0)
    summed_terms = lax.psum(vocab_sums, ("cand", "tensor"))
    own_terms = lax.dynamic_slice_in_dim(summed_terms, cand_id * length, length, 1)
    mask_values = loss_mask.astype(jnp.float32)
    token_loss = mask_values * (jnp.log(own_terms[0]) - own_terms[1])
    onehot = (chosen == jnp.arange(CANDS)).astype(jnp.float32)
    loss_sums, counts = lax.psum(
        (onehot * jnp.sum(token_loss), onehot * jnp.sum(mask_values)), "cand"
    )
    return (token_loss, loss_sums / jnp.maximum(counts, 1.0))


def solution(mesh):
    in_specs = (
        P("cand", None),
        P(),
        P("cand"),
        P(),
        P(),
        P("cand", "tensor"),
        P(None, "cand", "tensor"),
        P("cand", None),
        P(None, "cand", None),
        P("cand", None),
        P(None, "cand", None),
        P("tensor", "cand"),
        P(None, "tensor", "cand"),
        P(),
        P(),
        P(),
        P(None, ("cand", "tensor")),
    )
    out_specs = (P("cand"), P())
    return jax.shard_map(
        on_device, mesh=mesh, in_specs=in_specs, out_specs=out_specs, check_vma=False
    )
```

profile of v0, /device:TPU:0, one launch (start us, length us, event | category | flops | bytes accessed | tf_op | source)
XLA Modules:
  0.0 451.5 jit_solution(439209231556427896)
XLA Ops:
  7.2 1.9 constant_dynamic-slice_fusion.1
  9.2 2.3 dynamic-slice_reduce_fusion
  13.8 1.8 constant_dynamic-slice_fusion.2
  15.7 2.4 dynamic-slice_reduce_fusion.1
  24.3 9.1 %all-gather.14.cloned.1.call-done = bf16[3584,256]{1,0:T(8,128)(2,1)} async-done(((bf16[896,256]{1,0:T(8,128)(2,1)}), bf16[3584,256]{1,0:T(8,128)(2,1)}) %all-gather.14.cloned.1.call-update) | async-done | bytes 1835024 | tf_op jit(solution)/shard_map/all_gather | solution.py:74
  33.4 22.7 %all-gather.16.cloned.1.call-done = bf16[3584,256]{1,0:T(8,128)(2,1)} async-done(((bf16[896,256]{1,0:T(8,128)(2,1)}), bf16[3584,256]{1,0:T(8,128)(2,1)}) %all-gather.16.cloned.1.call-update) | async-done | bytes 1835024 | tf_op jit(solution)/shard_map/all_gather | solution.py:78
  56.1 3.6 fusion.20
  60.0 29.2 %all-gather.20.cloned.1.call-done = bf16[3584,512]{1,0:T(8,128)(2,1)} async-done(((bf16[896,512]{1,0:T(8,128)(2,1)}), bf16[3584,512]{1,0:T(8,128)(2,1)}) %all-gather.20.cloned.1.call-update) | async-done | bytes 3670032 | tf_op jit(solution)/shard_map/all_gather | solution.py:77
  89.2 32.9 %all-gather.18.cloned.1.call-done = bf16[3584,512]{1,0:T(8,128)(2,1)} async-done(((bf16[896,512]{1,0:T(8,128)(2,1)}), bf16[3584,512]{1,0:T(8,128)(2,1)}) %all-gather.18.cloned.1.call-update) | async-done | bytes 3670032 | tf_op jit(solution)/shard_map/all_gather | solution.py:73
  122.1 5.2 %fusion = f32[128,512]{1,0:T(8,128)S(1)} fusion(bf16[3584,512]{1,0:T(8,128)(2,1)} %all-gather.20.cloned.1.call-done, bf16[3584,512]{1,0:T(8,128)(2,1)} %all-gather.18.cloned.1.call-done, f32[]{:T(128)} %bitcast.1, bf16[128,3584]{1,0:T(8,128)(2,1)S(1)} %copy-done.1, f32[3584]{0:T(1024)S(1)} %copy-done.8, f32[128]{0:T(128)S(1)} %add_rsqrt_fusion.2), kind=kOutput, calls=%fused_computation.6 | convolution fusion | flops 480772096 | bytes 8534532 | tf_op jit(solution)/shard_map/dot_general | solution.py:91
  127.9 16.7 %all-gather.10.cloned.1.call-done = bf16[3584,256]{1,0:T(8,128)(2,1)} async-done(((bf16[896,256]{1,0:T(8,128)(2,1)}), bf16[3584,256]{1,0:T(8,128)(2,1)}) %all-gather.10.cloned.1.call-update) | async-done | bytes 1835024 | tf_op jit(solution)/shard_map/all_gather | solution.py:75
  144.6 22.5 %all-gather.12.cloned.1.call-done = bf16[3584,256]{1,0:T(8,128)(2,1)} async-done(((bf16[896,256]{1,0:T(8,128)(2,1)}), bf16[3584,256]{1,0:T(8,128)(2,1)}) %all-gather.12.cloned.1.call-update) | async-done | bytes 1835024 | tf_op jit(solution)/shard_map/all_gather | solution.py:79
  167.2 3.9 convolution_convert_fusion
  171.1 29.1 %all-gather.24.cloned.1.call-done = bf16[512,3584]{1,0:T(8,128)(2,1)} async-done(((bf16[512,896]{1,0:T(8,128)(2,1)}), bf16[512,3584]{1,0:T(8,128)(2,1)}) %all-gather.24.cloned.1.call-update) | async-done | bytes 3670032 | tf_op jit(solution)/shard_map/all_gather | solution.py:80
  200.2 33.1 %all-gather.22.cloned.1.call-done = bf16[512,3584]{1,0:T(8,128)(2,1)} async-done(((bf16[512,896]{1,0:T(8,128)(2,1)}), bf16[512,3584]{1,0:T(8,128)(2,1)}) %all-gather.22.cloned.1.call-update) | async-done | bytes 3670032 | tf_op jit(solution)/shard_map/all_gather | solution.py:76
  233.3 6.6 %fusion.1 = f32[128,3584]{1,0:T(8,128)} fusion(bf16[128,512]{0,1:T(8,128)(2,1)S(1)} %bitcast.38, bf16[512,3584]{1,0:T(8,128)(2,1)} %all-gather.24.cloned.1.call-done, bf16[512,3584]{1,0:T(8,128)(2,1)} %all-gather.22.cloned.1.call-done, f32[]{:T(128)} %bitcast.1), kind=kOutput, calls=%fused_computation.7 | convolution fusion | flops 478937088 | bytes 9306116 | tf_op jit(solution)/shard_map/dot_general | solution.py:111
  240.2 95.7 %all-reduce.3.cloned.1.call-done = f32[128,3584]{1,0:T(8,128)} async-done(((f32[128,3584]{1,0:T(8,128)}), f32[128,3584]{1,0:T(8,128)}) %all-reduce.3.cloned.1.call-update) | async-done | bytes 1835024 | tf_op jit(solution)/shard_map/psum | solution.py:115
  335.9 1.8 multiply_reduce_fusion.1
  337.8 2.0 multiply_reduce_fusion
  341.3 31.1 %all-gather.26.cloned.1.call-done = bf16[512,3584]{1,0:T(8,128)(2,1)} async-done(((bf16[128,3584]{1,0:T(8,128)(2,1)}), bf16[512,3584]{1,0:T(8,128)(2,1)}) %all-gather.26.cloned.1.call-update) | async-done | bytes 3670032 | tf_op jit(solution)/shard_map/all_gather | solution.py:118
  372.4 22.9 %exponential_reduce_fusion = (f32[512]{0:T(512)S(1)}, f32[512]{0:T(512)S(1)}) fusion(s32[512]{0:T(512)S(1)} %broadcast_subtract_fusion, bf16[512,3584]{1,0:T(8,128)(2,1)} %all-gather.26.cloned.1.call-done, bf16[3584,4096]{1,0:T(8,128)(2,1)} %param.33), kind=kOutput, calls=%fused_computation.2 | convolution fusion | flops 15044968448 | bytes 33036288 | tf_op jit(solution)/shard_map/dot_general | solution.py:117
  395.3 39.3 %psum.29 = f32[2,512]{1,0:T(2,128)S(1)} all-reduce(f32[2,512]{1,0:T(2,128)S(1)} %pad_maximum_fusion), channel_id=1, replica_groups=mesh['cand'=4,'tensor'=8] {'cand','tensor'}, use_global_device_ids=true, to_apply=%region_11.12 | all-reduce | flops 1024 | bytes 8192 | tf_op jit(solution)/shard_map/psum | solution.py:128
  435.8 1.8 compare_select_fusion
  437.6 6.5 %all-reduce = (f32[4]{0:T(128)S(1)}, f32[4]{0:T(128)S(1)}) all-reduce(f32[4]{0:T(128)S(1)} %get-tuple-element.18, f32[4]{0:T(128)S(1)} %get-tuple-element.17), channel_id=1, replica_groups=mesh['cand'=4,'tensor'=8] {'cand'}, use_global_device_ids=true, to_apply=%region_13.14 | all-reduce | flops 8 | bytes 64 | tf_op jit(solution)/shard_map/psum | solution.py:133
  (65 shorter events, 10.8 us)
Async XLA Ops:
  7.2 4.4 copy-start.2
  7.2 26.2 %all-gather.14.cloned.1.call-start = ((), (), s32[]{:S(2)}) async-start(), calls=%async_computation.2 | async-start | bytes 2293760 | tf_op jit(solution)/shard_map/all_gather | solution.py:74
  9.2 46.9 %all-gather.16.cloned.1.call-start = ((), (), s32[]{:S(2)}) async-start(), calls=%async_computation.3 | async-start | bytes 2293760 | tf_op jit(solution)/shard_map/all_gather | solution.py:78
  11.6 77.6 %all-gather.20.cloned.1.call-start = ((), (), s32[]{:S(2)}) async-start(), calls=%async_computation.5 | async-start | bytes 4587520 | tf_op jit(solution)/shard_map/all_gather | solution.py:77
  13.2 5.0 %copy-start.3 = (bf16[2,512,896]{2,1,0:T(8,128)(2,1)S(1)}, bf16[2,512,896]{2,1,0:T(8,128)(2,1)}, u32[]{:S(2)}) copy-start(bf16[2,512,896]{2,1,0:T(8,128)(2,1)} %param.29) | copy-start | bytes 5505028
  13.2 108.9 %all-gather.18.cloned.1.call-start = ((), (), s32[]{:S(2)}) async-start(), calls=%async_computation.4 | async-start | bytes 4587520 | tf_op jit(solution)/shard_map/all_gather | solution.py:73
  13.8 130.9 %all-gather.10.cloned.1.call-start = ((), (), s32[]{:S(2)}) async-start(), calls=%async_computation | async-start | bytes 2293760 | tf_op jit(solution)/shard_map/all_gather | solution.py:75
  15.6 4.9 %copy-start.9 = (s32[4]{0:T(128)S(1)}, s32[4]{0:T(128)}, u32[]{:S(2)}) copy-start(s32[4]{0:T(128)} %param.20) | copy-start | bytes 52
  15.6 7.4 %copy-start.10 = (f32[4]{0:T(128)S(1)}, f32[4]{0:T(128)}, u32[]{:S(2)}) copy-start(f32[4]{0:T(128)} %param.21) | copy-start | bytes 52
  15.7 8.1 %copy-start.1 = (bf16[128,3584]{1,0:T(8,128)(2,1)S(1)}, bf16[128,3584]{1,0:T(8,128)(2,1)}, u32[]{:S(2)}) copy-start(bf16[128,3584]{1,0:T(8,128)(2,1)} %param.17) | copy-start | bytes 2752516
  15.7 40.4 %copy-start.8 = (f32[3584]{0:T(1024)S(1)}, f32[3584]{0:T(1024)}, u32[]{:S(2)}) copy-start(f32[3584]{0:T(1024)} %param.30) | copy-start | bytes 43012
  15.7 151.5 %all-gather.12.cloned.1.call-start = ((), (), s32[]{:S(2)}) async-start(), calls=%async_computation.1 | async-start | bytes 2293760 | tf_op jit(solution)/shard_map/all_gather | solution.py:79
  18.2 182.1 %all-gather.24.cloned.1.call-start = ((), (), s32[]{:S(2)}) async-start(), calls=%async_computation.7 | async-start | bytes 4587520 | tf_op jit(solution)/shard_map/all_gather | solution.py:80
  19.7 213.6 %all-gather.22.cloned.1.call-start = ((), (), s32[]{:S(2)}) async-start(), calls=%async_computation.6 | async-start | bytes 4587520 | tf_op jit(solution)/shard_map/all_gather | solution.py:76
  20.5 315.4 %all-reduce.3.cloned.1.call-start = ((), (), s32[]{:S(2)}) async-start(), calls=%async_computation.8 | async-start | bytes 3670016 | tf_op jit(solution)/shard_map/psum | solution.py:115
  239.9 97.8 %copy-start.4 = (f32[3584]{0:T(1024)S(1)}, f32[3584]{0:T(1024)}, u32[]{:S(2)}) copy-start(f32[3584]{0:T(1024)} %param.31) | copy-start | bytes 43012
  239.9 99.9 %copy-start.5 = (f32[3584]{0:T(1024)S(1)}, f32[3584]{0:T(1024)}, u32[]{:S(2)}) copy-start(f32[3584]{0:T(1024)} %param.32) | copy-start | bytes 43012
  239.9 132.5 %all-gather.26.cloned.1.call-start = ((), (), s32[]{:S(2)}) async-start(), calls=%async_computation.9 | async-start | bytes 4587520 | tf_op jit(solution)/shard_map/all_gather | solution.py:118
  335.9 3.9 copy-start
  337.8 3.5 copy-start.6
  341.3 93.4 %copy-start.7 = (s32[128]{0:T(128)S(1)}, s32[128]{0:T(128)}, u32[]{:S(2)}) copy-start(s32[128]{0:T(128)} %param.19) | copy-start | bytes 1540
Sparse Core Ops, SparseCore 0:
  9.5 23.8 all-gather.13
  35.0 21.0 all-gather.15
  57.7 31.4 all-gather.19
  90.6 31.4 all-gather.17
  123.5 21.0 all-gather.9
  146.1 21.0 all-gather.11
  168.7 31.4 all-gather.23
  201.8 31.4 all-gather.21
  240.1 95.7 all-reduce.2
  341.4 30.9 all-gather.25
where the time goes:
time: 452 us
  waiting for transfers between devices  324 us (72%)
  blocking collectives  45.9 us (10%)
  matrix products  42.5 us (9%)
  other arithmetic  17.5 us (4%)
  between operations  16.3 us (4%)
  local copies, waits for them, and re-layouts  5.26 us (1%)
    psum x1, waiting for transfers between devices, on_device(): attended = lax.psum(partial_value, 'tensor')  95.7 us
    psum x1, blocking collectives, on_device(): summed_terms = lax.psum(vocab_sums, ('cand', 'tensor'))  39.3 us
    all_gather x1, waiting for transfers between devices, on_device(): lax.all_gather(base_o, 'cand', axis=1, tiled=True)  33.1 us
    all_gather x1, waiting for transfers between devices, on_device(): lax.all_gather(base_q, 'cand', axis=0, tiled=True)  32.9 us
    all_gather x1, waiting for transfers between devices, on_device(): lax.all_gather(final_rows, 'cand', axis=0, tiled=True)  31.1 us
    all_gather x1, waiting for transfers between devices, on_device(): lax.all_gather(summed[0], 'cand', axis=0, tiled=True)  29.2 us
    all_gather x1, waiting for transfers between devices, on_device(): lax.all_gather(summed[3], 'cand', axis=1, tiled=True)  29.1 us
    dot_general x1, matrix products, on_device(): jnp.dot(lax.all_gather(final_rows, 'cand', axis=0, tiled=True), unembed,...  22.9 us
  transfers between devices with their start and end apart: 10, of which 10 were waited for; matrix products, arithmetic and copies ran while one was open for 6% of the time, Pallas kernels for 0%

commit v1 on v0

--- a/solution.py
+++ b/solution.py
@@ -125,7 +125,9 @@
     matches = local_ids[:, None] == vocab_index[None, :]
     picked = jnp.sum(jnp.where(matches, capped, 0.0), axis=1)
     vocab_sums = jnp.stack([totals, picked], axis=0)
-    summed_terms = lax.psum(vocab_sums, ("cand", "tensor"))
+    summed_terms = vocab_sums
+    for axis in ("tensor", "cand"):
+        summed_terms = lax.psum(summed_terms, axis)
     own_terms = lax.dynamic_slice_in_dim(summed_terms, cand_id * length, length, 1)
     mask_values = loss_mask.astype(jnp.float32)
     token_loss = mask_values * (jnp.log(own_terms[0]) - own_terms[1])

time: 452 us -> 439 us (0.971)
  blocking collectives: 45.9 us -> 33.1 us
    psum x1 -> x2, blocking collectives: 39.3 us -> 27.3 us  [on_device(): summed_terms = lax.psum(summed_terms, axis)]
where the time goes in v1:
time: 439 us
  waiting for transfers between devices  324 us (74%)
  matrix products  42.5 us (10%)
  blocking collectives  33.1 us (8%)
  other arithmetic  17.6 us (4%)
  between operations  16.3 us (4%)
  local copies, waits for them, and re-layouts  5.25 us (1%)
    psum x1, waiting for transfers between devices, on_device(): attended = lax.psum(partial_value, 'tensor')  95.7 us
    all_gather x1, waiting for transfers between devices, on_device(): lax.all_gather(base_o, 'cand', axis=1, tiled=True)  33.1 us
    all_gather x1, waiting for transfers between devices, on_device(): lax.all_gather(base_q, 'cand', axis=0, tiled=True)  32.9 us
    all_gather x1, waiting for transfers between devices, on_device(): lax.all_gather(final_rows, 'cand', axis=0, tiled=True)  31.1 us
    all_gather x1, waiting for transfers between devices, on_device(): lax.all_gather(summed[0], 'cand', axis=0, tiled=True)  29.2 us
    all_gather x1, waiting for transfers between devices, on_device(): lax.all_gather(summed[3], 'cand', axis=1, tiled=True)  29.1 us
    psum x2, blocking collectives, on_device(): summed_terms = lax.psum(summed_terms, axis)  27.3 us
    dot_general x1, matrix products, on_device(): jnp.dot(lax.all_gather(final_rows, 'cand', axis=0, tiled=True), unembed,...  22.9 us
  transfers between devices with their start and end apart: 10, of which 10 were waited for; matrix products, arithmetic and copies ran while one was open for 6% of the time, Pallas kernels for 0%

profile of v1, /device:TPU:0, one launch (start us, length us, event | category | flops | bytes accessed | tf_op | source)
XLA Modules:
  0.0 438.9 jit_solution(14010259344181664347)
XLA Ops:
  7.2 1.9 constant_dynamic-slice_fusion.1
  9.2 2.3 dynamic-slice_reduce_fusion
  15.7 2.4 dynamic-slice_reduce_fusion.1
  24.3 9.1 %all-gather.14.cloned.1.call-done = bf16[3584,256]{1,0:T(8,128)(2,1)} async-done(((bf16[896,256]{1,0:T(8,128)(2,1)}), bf16[3584,256]{1,0:T(8,128)(2,1)}) %all-gather.14.cloned.1.call-update) | async-done | bytes 1835024 | tf_op jit(solution)/shard_map/all_gather | solution.py:74
  33.4 22.7 %all-gather.16.cloned.1.call-done = bf16[3584,256]{1,0:T(8,128)(2,1)} async-done(((bf16[896,256]{1,0:T(8,128)(2,1)}), bf16[3584,256]{1,0:T(8,128)(2,1)}) %all-gather.16.cloned.1.call-update) | async-done | bytes 1835024 | tf_op jit(solution)/shard_map/all_gather | solution.py:78
  56.1 3.6 fusion.20
  60.0 29.2 %all-gather.20.cloned.1.call-done = bf16[3584,512]{1,0:T(8,128)(2,1)} async-done(((bf16[896,512]{1,0:T(8,128)(2,1)}), bf16[3584,512]{1,0:T(8,128)(2,1)}) %all-gather.20.cloned.1.call-update) | async-done | bytes 3670032 | tf_op jit(solution)/shard_map/all_gather | solution.py:77
  89.2 32.9 %all-gather.18.cloned.1.call-done = bf16[3584,512]{1,0:T(8,128)(2,1)} async-done(((bf16[896,512]{1,0:T(8,128)(2,1)}), bf16[3584,512]{1,0:T(8,128)(2,1)}) %all-gather.18.cloned.1.call-update) | async-done | bytes 3670032 | tf_op jit(solution)/shard_map/all_gather | solution.py:73
  122.1 5.2 %fusion = f32[128,512]{1,0:T(8,128)S(1)} fusion(bf16[3584,512]{1,0:T(8,128)(2,1)} %all-gather.20.cloned.1.call-done, bf16[3584,512]{1,0:T(8,128)(2,1)} %all-gather.18.cloned.1.call-done, f32[]{:T(128)} %bitcast.1, bf16[128,3584]{1,0:T(8,128)(2,1)S(1)} %copy-done.1, f32[3584]{0:T(1024)S(1)} %copy-done.8, f32[128]{0:T(128)S(1)} %add_rsqrt_fusion.2), kind=kOutput, calls=%fused_computation.6 | convolution fusion | flops 480772096 | bytes 8534532 | tf_op jit(solution)/shard_map/dot_general | solution.py:91
  127.9 16.7 %all-gather.10.cloned.1.call-done = bf16[3584,256]{1,0:T(8,128)(2,1)} async-done(((bf16[896,256]{1,0:T(8,128)(2,1)}), bf16[3584,256]{1,0:T(8,128)(2,1)}) %all-gather.10.cloned.1.call-update) | async-done | bytes 1835024 | tf_op jit(solution)/shard_map/all_gather | solution.py:75
  144.6 22.5 %all-gather.12.cloned.1.call-done = bf16[3584,256]{1,0:T(8,128)(2,1)} async-done(((bf16[896,256]{1,0:T(8,128)(2,1)}), bf16[3584,256]{1,0:T(8,128)(2,1)}) %all-gather.12.cloned.1.call-update) | async-done | bytes 1835024 | tf_op jit(solution)/shard_map/all_gather | solution.py:79
  167.2 3.9 convolution_convert_fusion
  171.1 29.1 %all-gather.24.cloned.1.call-done = bf16[512,3584]{1,0:T(8,128)(2,1)} async-done(((bf16[512,896]{1,0:T(8,128)(2,1)}), bf16[512,3584]{1,0:T(8,128)(2,1)}) %all-gather.24.cloned.1.call-update) | async-done | bytes 3670032 | tf_op jit(solution)/shard_map/all_gather | solution.py:80
  200.2 33.1 %all-gather.22.cloned.1.call-done = bf16[512,3584]{1,0:T(8,128)(2,1)} async-done(((bf16[512,896]{1,0:T(8,128)(2,1)}), bf16[512,3584]{1,0:T(8,128)(2,1)}) %all-gather.22.cloned.1.call-update) | async-done | bytes 3670032 | tf_op jit(solution)/shard_map/all_gather | solution.py:76
  233.3 6.6 %fusion.1 = f32[128,3584]{1,0:T(8,128)} fusion(bf16[128,512]{0,1:T(8,128)(2,1)S(1)} %bitcast.38, bf16[512,3584]{1,0:T(8,128)(2,1)} %all-gather.24.cloned.1.call-done, bf16[512,3584]{1,0:T(8,128)(2,1)} %all-gather.22.cloned.1.call-done, f32[]{:T(128)} %bitcast.1), kind=kOutput, calls=%fused_computation.7 | convolution fusion | flops 478937088 | bytes 9306116 | tf_op jit(solution)/shard_map/dot_general | solution.py:111
  240.2 95.7 %all-reduce.3.cloned.1.call-done = f32[128,3584]{1,0:T(8,128)} async-done(((f32[128,3584]{1,0:T(8,128)}), f32[128,3584]{1,0:T(8,128)}) %all-reduce.3.cloned.1.call-update) | async-done | bytes 1835024 | tf_op jit(solution)/shard_map/psum | solution.py:115
  335.9 1.8 multiply_reduce_fusion.1
  337.8 2.0 multiply_reduce_fusion
  341.3 31.1 %all-gather.26.cloned.1.call-done = bf16[512,3584]{1,0:T(8,128)(2,1)} async-done(((bf16[128,3584]{1,0:T(8,128)(2,1)}), bf16[512,3584]{1,0:T(8,128)(2,1)}) %all-gather.26.cloned.1.call-update) | async-done | bytes 3670032 | tf_op jit(solution)/shard_map/all_gather | solution.py:118
  372.4 22.9 %exponential_reduce_fusion = (f32[512]{0:T(512)S(1)}, f32[512]{0:T(512)S(1)}) fusion(s32[512]{0:T(512)S(1)} %broadcast_subtract_fusion, bf16[512,3584]{1,0:T(8,128)(2,1)} %all-gather.26.cloned.1.call-done, bf16[3584,4096]{1,0:T(8,128)(2,1)} %param.33), kind=kOutput, calls=%fused_computation.2 | convolution fusion | flops 15044968448 | bytes 33036288 | tf_op jit(solution)/shard_map/dot_general | solution.py:117
  395.3 21.4 %psum.36 = f32[2,512]{1,0:T(2,128)S(1)} all-reduce(f32[2,512]{1,0:T(2,128)S(1)} %pad_maximum_fusion), channel_id=1, replica_groups=mesh['cand'=4,'tensor'=8] {'tensor'}, use_global_device_ids=true, to_apply=%region_11.12 | all-reduce | flops 1024 | bytes 8192 | tf_op jit(solution)/shard_map/psum | solution.py:130
  416.7 5.9 %psum.37 = f32[2,512]{1,0:T(2,128)S(1)} all-reduce(f32[2,512]{1,0:T(2,128)S(1)} %psum.36), channel_id=1, replica_groups=mesh['cand'=4,'tensor'=8] {'cand'}, use_global_device_ids=true, to_apply=%region_12.13 | all-reduce | flops 1024 | bytes 8192 | tf_op jit(solution)/shard_map/psum | solution.py:130
  423.8 1.9 compare_select_fusion
  425.7 5.8 %all-reduce = (f32[4]{0:T(128)S(1)}, f32[4]{0:T(128)S(1)}) all-reduce(f32[4]{0:T(128)S(1)} %get-tuple-element.18, f32[4]{0:T(128)S(1)} %get-tuple-element.17), channel_id=1, replica_groups=mesh['cand'=4,'tensor'=8] {'cand'}, use_global_device_ids=true, to_apply=%region_14.15 | all-reduce | flops 8 | bytes 64 | tf_op jit(solution)/shard_map/psum | solution.py:135
  (66 shorter events, 12.7 us)
Async XLA Ops:
  7.2 4.4 %copy-start.2 = (bf16[2,896,512]{2,1,0:T(8,128)(2,1)S(1)}, bf16[2,896,512]{2,1,0:T(8,128)(2,1)}, u32[]{:S(2)}) copy-start(bf16[2,896,512]{2,1,0:T(8,128)(2,1)} %param.23) | copy-start | bytes 5505028
  7.2 26.2 %all-gather.14.cloned.1.call-start = ((), (), s32[]{:S(2)}) async-start(), calls=%async_computation.2 | async-start | bytes 2293760 | tf_op jit(solution)/shard_map/all_gather | solution.py:74
  9.2 46.9 %all-gather.16.cloned.1.call-start = ((), (), s32[]{:S(2)}) async-start(), calls=%async_computation.3 | async-start | bytes 2293760 | tf_op jit(solution)/shard_map/all_gather | solution.py:78
  11.5 77.6 %all-gather.20.cloned.1.call-start = ((), (), s32[]{:S(2)}) async-start(), calls=%async_computation.5 | async-start | bytes 4587520 | tf_op jit(solution)/shard_map/all_gather | solution.py:77
  13.1 5.0 %copy-start.3 = (bf16[2,512,896]{2,1,0:T(8,128)(2,1)S(1)}, bf16[2,512,896]{2,1,0:T(8,128)(2,1)}, u32[]{:S(2)}) copy-start(bf16[2,512,896]{2,1,0:T(8,128)(2,1)} %param.29) | copy-start | bytes 5505028
  13.2 108.9 %all-gather.18.cloned.1.call-start = ((), (), s32[]{:S(2)}) async-start(), calls=%async_computation.4 | async-start | bytes 4587520 | tf_op jit(solution)/shard_map/all_gather | solution.py:73
  13.7 130.9 %all-gather.10.cloned.1.call-start = ((), (), s32[]{:S(2)}) async-start(), calls=%async_computation | async-start | bytes 2293760 | tf_op jit(solution)/shard_map/all_gather | solution.py:75
  15.6 4.9 %copy-start.9 = (s32[4]{0:T(128)S(1)}, s32[4]{0:T(128)}, u32[]{:S(2)}) copy-start(s32[4]{0:T(128)} %param.20) | copy-start | bytes 52
  15.6 7.4 %copy-start.10 = (f32[4]{0:T(128)S(1)}, f32[4]{0:T(128)}, u32[]{:S(2)}) copy-start(f32[4]{0:T(128)} %param.21) | copy-start | bytes 52
  15.6 8.1 %copy-start.1 = (bf16[128,3584]{1,0:T(8,128)(2,1)S(1)}, bf16[128,3584]{1,0:T(8,128)(2,1)}, u32[]{:S(2)}) copy-start(bf16[128,3584]{1,0:T(8,128)(2,1)} %param.17) | copy-start | bytes 2752516
  15.6 40.5 %copy-start.8 = (f32[3584]{0:T(1024)S(1)}, f32[3584]{0:T(1024)}, u32[]{:S(2)}) copy-start(f32[3584]{0:T(1024)} %param.30) | copy-start | bytes 43012
  15.7 151.5 %all-gather.12.cloned.1.call-start = ((), (), s32[]{:S(2)}) async-start(), calls=%async_computation.1 | async-start | bytes 2293760 | tf_op jit(solution)/shard_map/all_gather | solution.py:79
  18.1 182.1 %all-gather.24.cloned.1.call-start = ((), (), s32[]{:S(2)}) async-start(), calls=%async_computation.7 | async-start | bytes 4587520 | tf_op jit(solution)/shard_map/all_gather | solution.py:80
  19.7 213.6 %all-gather.22.cloned.1.call-start = ((), (), s32[]{:S(2)}) async-start(), calls=%async_computation.6 | async-start | bytes 4587520 | tf_op jit(solution)/shard_map/all_gather | solution.py:76
  20.5 315.4 %all-reduce.3.cloned.1.call-start = ((), (), s32[]{:S(2)}) async-start(), calls=%async_computation.8 | async-start | bytes 3670016 | tf_op jit(solution)/shard_map/psum | solution.py:115
  239.9 97.8 %copy-start.4 = (f32[3584]{0:T(1024)S(1)}, f32[3584]{0:T(1024)}, u32[]{:S(2)}) copy-start(f32[3584]{0:T(1024)} %param.31) | copy-start | bytes 43012
  239.9 99.9 %copy-start.5 = (f32[3584]{0:T(1024)S(1)}, f32[3584]{0:T(1024)}, u32[]{:S(2)}) copy-start(f32[3584]{0:T(1024)} %param.32) | copy-start | bytes 43012
  239.9 132.5 %all-gather.26.cloned.1.call-start = ((), (), s32[]{:S(2)}) async-start(), calls=%async_computation.9 | async-start | bytes 4587520 | tf_op jit(solution)/shard_map/all_gather | solution.py:118
  335.9 3.9 copy-start
  337.8 3.5 copy-start.6
  341.3 81.4 %copy-start.7 = (s32[128]{0:T(128)S(1)}, s32[128]{0:T(128)}, u32[]{:S(2)}) copy-start(s32[128]{0:T(128)} %param.19) | copy-start | bytes 1540
Sparse Core Ops, SparseCore 0:
  9.5 23.8 all-gather.13
  35.0 21.0 all-gather.15
  57.7 31.4 all-gather.19
  90.6 31.4 all-gather.17
  123.5 21.0 all-gather.9
  146.1 21.0 all-gather.11
  168.7 31.4 all-gather.23
  201.8 31.4 all-gather.21
  240.1 95.7 all-reduce.2
  341.4 30.9 all-gather.25
